TPU v7x, 256 devices: a whole 4x4x8 slice. The times are simulated.
256 devices in a mesh: dp: 32 (over z, y), mp: 8 (over x, core).
Axes of the slice: x: 4, y: 4, z: 8, core: 2. Of those that a mesh axis runs over, the one named last changes fastest.
Arguments:
- queries: bfloat16 [4096, 8192], P('dp', 'mp'), may hold values from -8 to 8
- tree_keys: bfloat16 [4096, 1024], P('dp', 'mp'), may hold values from -18 to 18
- tree_values: bfloat16 [4096, 1024], P('dp', 'mp'), may hold values from -6 to 6
- cache_keys: bfloat16 [64, 4096, 1024], P('dp', None, 'mp'), may hold values from -8 to 8
- cache_values: bfloat16 [64, 4096, 1024], P('dp', None, 'mp'), may hold values from -6 to 6
- cache_lens: int32 [64], P('dp'), may hold values from 1024 to 4096, as said below
- parents: int32 [64, 64], P('dp'), may hold values from -1 to 62, as said below
- accepted_nodes: int32 [64, 8], P('dp'), may hold values from 0 to 63, as said below
- residual: bfloat16 [4096, 8192], P('dp', 'mp'), may hold values from -1.796875 to 1.796875
- out_weight: bfloat16 [8192, 8192], P('mp', 'dp'), may hold values from -0.0625 to 0.0625
Outputs:
- tree_hidden: bfloat16 [4096, 8192], P('dp', 'mp')
- accepted_hidden: bfloat16 [512, 8192], P(None, 'mp')
Inputs may be any that keep to these rules, and one draw needn't show every extreme that they name: parents[r, 0] = -1 and 0 <= parents[r, i] < i for i >= 1. accepted_nodes[r, 0] = 0, the nodes of a row increase, and parents[r, accepted_nodes[r, a + 1]] = accepted_nodes[r, a]. `cache_lens`: some request has exactly 4096 filled positions.
All inputs are finite; a program needn't handle non-finite values.
Results may differ from a plain program's by a relative error of at most 0.015.
Values may be sent and summed in bfloat16 or wider, within the bound.
A program may use at most 64 MiB of HBM per device.

v0:
```python
import math
import jax
import jax.numpy as jnp
from jax import lax
from jax.sharding import PartitionSpec as P

HEADS = 64
KV_HEADS = 8
HD = 128
neg_large = -1e30


def cut_along(value, dim, size):
    before, after = (value.shape[:dim], value.shape[dim + 1 :])
    return jnp.moveaxis(value.reshape(*before, size, -1, *after), dim, 0)


def summed_on_arrival(value, axis, dim):
    blocks = cut_along(value, dim, lax.axis_size(axis))
    arrived = lax.all_to_all(blocks, axis, split_axis=0, concat_axis=0, tiled=True)
    return arrived.astype(jnp.float32).sum(axis=0)


def sent_to_all(value, axis):
    size = lax.axis_size(axis)
    return lax.all_to_all(
        jnp.broadcast_to(value[None], (size, *value.shape)), axis, 0, 0, tiled=True
    )


def laid_out(blocks, dim):
    blocks = jnp.moveaxis(blocks, 0, dim)
    dims = blocks.shape
    return blocks.reshape(*dims[:dim], dims[dim] * dims[dim + 1], *dims[dim + 2 :])


def collect(value, axis, dim):
    blocks = sent_to_all(value, axis)
    return laid_out(blocks, dim)


def ancestry(parents, node_count):
    positions = jnp.arange(node_count, dtype=jnp.int32)
    parent_hot = (parents[:, :, None] == positions[None, None, :]).astype(jnp.float32)
    reached = parent_hot + jnp.eye(node_count, dtype=jnp.float32)[None]
    for squaring in range((node_count - 1).bit_length()):
        reached = jnp.minimum(
            jnp.einsum("rij,rjk->rik", reached, reached, precision=lax.Precision.HIGHEST), 1.0
        )
    return reached > 0.5


def per_device(
    queries,
    tree_keys,
    tree_values,
    cache_keys,
    cache_values,
    cache_lens,
    parents,
    accepted_nodes,
    residual,
    out_weight,
):
    request_count = parents.shape[0]
    node_count = parents.shape[1]
    cache_length = cache_keys.shape[1]
    kv_local = tree_keys.shape[1] // HD
    group_size = HEADS // KV_HEADS
    scale_factor = 1.0 / math.sqrt(HD)
    query_grid = queries.reshape(request_count, node_count, kv_local, group_size, HD)
    tree_key_grid = tree_keys.reshape(request_count, node_count, kv_local, HD)
    tree_value_grid = tree_values.reshape(request_count, node_count, kv_local, HD)
    cache_key_grid = cache_keys.reshape(request_count, cache_length, kv_local, HD)
    cache_value_grid = cache_values.reshape(request_count, cache_length, kv_local, HD)
    ancestor = ancestry(parents, node_count)
    tree_scores = (
        jnp.einsum(
            "rnkgd,rjkd->rnkgj", query_grid, tree_key_grid, preferred_element_type=jnp.float32
        )
        * scale_factor
    )
    tree_scores = jnp.where(ancestor[:, :, None, None, :], tree_scores, neg_large)
    run_max = jnp.max(tree_scores, axis=-1)
    tree_weights = jnp.exp(tree_scores - run_max[..., None])
    run_sum = jnp.sum(tree_weights, axis=-1)
    run_acc = jnp.einsum(
        "rnkgj,rjkd->rnkgd",
        tree_weights.astype(jnp.bfloat16),
        tree_value_grid,
        preferred_element_type=jnp.float32,
    )
    block_len = min(512, cache_length)

    def absorb(block_number, state_now):
        old_max, old_sum, old_acc = state_now
        block_start = block_number * block_len
        key_block = lax.dynamic_slice_in_dim(cache_key_grid, block_start, block_len, 1)
        value_block = lax.dynamic_slice_in_dim(cache_value_grid, block_start, block_len, 1)
        block_scores = (
            jnp.einsum(
                "rnkgd,rpkd->rnkgp", query_grid, key_block, preferred_element_type=jnp.float32
            )
            * scale_factor
        )
        positions = block_start + jnp.arange(block_len, dtype=jnp.int32)
        live_keys = positions[None, :] < cache_lens[:, None]
        block_scores = jnp.where(live_keys[:, None, None, None, :], block_scores, neg_large)
        new_max = jnp.maximum(old_max, jnp.max(block_scores, axis=-1))
        block_weights = jnp.exp(block_scores - new_max[..., None])
        rescale = jnp.exp(old_max - new_max)
        new_sum = old_sum * rescale + jnp.sum(block_weights, axis=-1)
        new_acc = old_acc * rescale[..., None] + jnp.einsum(
            "rnkgp,rpkd->rnkgd",
            block_weights.astype(jnp.bfloat16),
            value_block,
            preferred_element_type=jnp.float32,
        )
        return (new_max, new_sum, new_acc)

    trip_count = cache_length // block_len
    run_max, run_sum, run_acc = lax.fori_loop(0, trip_count, absorb, (run_max, run_sum, run_acc))
    attended = (run_acc / run_sum[..., None]).astype(jnp.bfloat16)
    attended = attended.reshape(request_count * node_count, kv_local * group_size * HD)
    partial_sum = jnp.dot(
        attended,
        lax.all_gather(out_weight, "dp", axis=1, tiled=True),
        preferred_element_type=jnp.float32,
    )
    own_share = summed_on_arrival(partial_sum.astype(jnp.bfloat16), "mp", 1)
    tree_hidden = (residual.astype(jnp.float32) + own_share).astype(jnp.bfloat16)
    row_base = jnp.arange(request_count, dtype=jnp.int32)[:, None] * node_count
    picked_rows = (row_base + accepted_nodes).reshape(-1)
    picked_hidden = jnp.take(tree_hidden, picked_rows, axis=0)
    accepted_hidden = collect(picked_hidden, "dp", 0)
    return (tree_hidden, accepted_hidden)


def solution(mesh):
    placed = (
        P("dp", "mp"),
        P("dp", "mp"),
        P("dp", "mp"),
        P("dp", None, "mp"),
        P("dp", None, "mp"),
        P("dp"),
        P("dp", None),
        P("dp", None),
        P("dp", "mp"),
        P("mp", "dp"),
    )
    return jax.shard_map(
        per_device,
        mesh=mesh,
        in_specs=placed,
        out_specs=(P("dp", "mp"), P(None, "mp")),
        check_vma=False,
    )
```

profile of v0, /device:TPU:8, one launch (start us, length us, event | category | flops | bytes accessed | tf_op | source)
XLA Modules:
  0.0 246.2 jit_solution(12301007341857706381)
XLA Ops:
  8.9 1.0 convolution_minimum_fusion.5
  12.2 31.6 %while.17 = (s32[]{:T(128)}, f32[2,64,1,8]{1,3,0,2:T(8,128)S(1)}, f32[2,64,1,8]{1,3,0,2:T(8,128)S(1)}, f32[2,64,1,8,128]{4,1,3,0,2:T(8,128)S(1)}, s32[2]{0:T(128...) while((s32[]{:T(128)}, f32[2,64,1,8]{1,3,0,2:T(8,128)S(1)}, ...), condition=%wide.region_5.6_spmd, body=%wide.region_2.5_spmd.sunk | while | flops 274469376 | bytes 8200375 | solution.py:122
  12.3 1.5 bitcast_reduce_fusion.2
  13.8 1.7 fusion.60
  16.3 1.5 bitcast_reduce_fusion.2
  17.8 1.7 fusion.60
  20.2 1.5 bitcast_reduce_fusion.2
  21.7 1.7 fusion.60
  24.2 1.5 bitcast_reduce_fusion.2
  25.7 1.7 fusion.60
  28.1 1.5 bitcast_reduce_fusion.2
  29.6 1.7 fusion.60
  32.1 1.5 bitcast_reduce_fusion.2
  33.6 1.7 fusion.60
  36.0 1.5 bitcast_reduce_fusion.2
  37.5 1.7 fusion.60
  40.0 1.5 bitcast_reduce_fusion.2
  41.5 1.7 fusion.60
  44.2 117.2 %all-gather.2.cloned.1.call-done = bf16[1024,8192]{1,0:T(8,128)(2,1)} async-done(((bf16[1024,256]{1,0:T(8,128)(2,1)}), bf16[1024,8192]{1,0:T(8,128)(2,1)}) %all-gather.2.cloned.1.call-update) | async-done | bytes 16777232 | tf_op jit(solution)/shard_map/all_gather | solution.py:127
  161.5 8.1 %convolution_convert_fusion = bf16[128,8192]{1,0:T(8,128)(2,1)S(1)} fusion(bf16[1024,8192]{1,0:T(8,128)(2,1)} %all-gather.2.cloned.1.call-done, bf16[16,8,8,128]{3,2,1,0:T(8,128)(2,1)S(1)} %bitcast.164), kind=kOutput, calls=%fused_computation.30 | convolution fusion | flops 2148532224 | bytes 19136512 | tf_op jit(solution)/shard_map/dot_general | solution.py:125
  169.6 1.5 copy.46
  171.1 4.4 %all-to-all-start = ((bf16[8,128,1024]{2,1,0:T(8,128)(2,1)}), bf16[8,128,1024]{2,1,0:T(8,128)(2,1)S(1)}, u32[]{:S(2)}, u32[]{:S(2)}) async-start(bf16[8,128,1024]{2,1,0:T(8,128)(2,1)} %bitcast.157), calls=%async_computation | async-start | bytes 4194304 | tf_op jit(solution)/shard_map/all_to_all | solution.py:20
  175.8 26.9 %all-to-all-done = bf16[8,128,1024]{2,1,0:T(8,128)(2,1)S(1)} async-done(((bf16[8,128,1024]{2,1,0:T(8,128)(2,1)}), bf16[8,128,1024]{2,1,0:T(8,128)(2,1)S(1)}, u32[]{:S(2)}, u32[]{:S(2)}) %all-to-all-start) | async-done | bytes 2097184 | tf_op jit(solution)/shard_map/all_to_all | solution.py:20
  203.9 34.5 %all_to_all.10 = bf16[32,16,1024]{2,1,0:T(8,128)(2,1)S(1)} all-to-all(bf16[32,16,1024]{2,1,0:T(8,128)(2,1)S(1)} %broadcast_in_dim.78), channel_id=1, replica_groups=mesh['dp'=32,'mp'=8] {'dp'}, dimensions={0} | all-to-all | bytes 2097152 | tf_op jit(solution)/shard_map/all_to_all | solution.py:26
  (91 shorter events, 12.6 us)
Async XLA Ops:
  7.2 4.7 %copy-start = (bf16[128,128]{1,0:T(8,128)(2,1)S(1)}, bf16[128,128]{1,0:T(8,128)(2,1)}, u32[]{:S(2)}) copy-start(bf16[128,128]{1,0:T(8,128)(2,1)} %param.14) | copy-start | bytes 98308
  7.2 3.9 %copy-start.3 = (bf16[128,128]{1,0:T(8,128)(2,1)S(1)}, bf16[128,128]{1,0:T(8,128)(2,1)}, u32[]{:S(2)}) copy-start(bf16[128,128]{1,0:T(8,128)(2,1)} %param.13) | copy-start | bytes 98308
  7.2 154.3 %all-gather.2.cloned.1.call-start = ((), (), s32[]{:S(2)}) async-start(), calls=%async_computation.2 | async-start | bytes 17301504 | tf_op jit(solution)/shard_map/all_gather | solution.py:127
  11.1 1.1 copy-start.4
  171.1 4.4 %copy-start.5 = (s32[2,8]{1,0:T(2,128)S(1)}, s32[2,8]{1,0:T(2,128)}, u32[]{:S(2)}) copy-start(s32[2,8]{1,0:T(2,128)} %param.19) | copy-start | bytes 196
  171.1 31.6 %all-to-all-start = ((bf16[8,128,1024]{2,1,0:T(8,128)(2,1)}), bf16[8,128,1024]{2,1,0:T(8,128)(2,1)S(1)}, u32[]{:S(2)}, u32[]{:S(2)}) async-start(bf16[8,128,1024]{2,1,0:T(8,128)(2,1)} %bitcast.157), calls=%async_computation | async-start | bytes 4194304 | tf_op jit(solution)/shard_map/all_to_all | solution.py:20
  175.5 27.5 %copy-start.2 = (bf16[128,1024]{1,0:T(8,128)(2,1)S(1)}, bf16[128,1024]{1,0:T(8,128)(2,1)}, u32[]{:S(2)}) copy-start(bf16[128,1024]{1,0:T(8,128)(2,1)} %param.20) | copy-start | bytes 786436
  203.1 36.3 %copy-start.1 = (bf16[128,1024]{1,0:T(8,128)(2,1)}, bf16[128,1024]{1,0:T(8,128)(2,1)S(1)}, u32[]{:S(2)}) copy-start(bf16[128,1024]{1,0:T(8,128)(2,1)S(1)} %add_convert_fusion) | copy-start | bytes 786436
Sparse Core Ops, SparseCore 0:
  10.5 150.9 all-gather.1
where the time goes:
time: 247 us; the launch traced here: 246 us
  waiting for transfers between devices  145 us (59%)
  matrix products  36 us (15%)
  blocking collectives  34.5 us (14%)
  between operations  14.3 us (6%)
  other arithmetic  6.76 us (3%)
  local copies, waits for them, and re-layouts  5.06 us (2%)
  starting transfers between devices  4.42 us (2%)
    all_gather x1, waiting for transfers between devices, per_device(): lax.all_gather(out_weight, 'dp', axis=1, tiled=True)  117 us
    all_to_all x1, blocking collectives, sent_to_all(): lax.all_to_all(jnp.broadcast_to(value[None], (size, *value.shape)), axis,...  34.5 us
    all_to_all x1, waiting for transfers between devices, summed_on_arrival(): lax.all_to_all(blocks, axis, split_axis=0, concat_axis=0, tiled=True)  26.9 us
    dot_general x8, matrix products, absorb(): jnp.einsum('rnkgp,rpkd->rnkgd', block_weights.astype(jnp.bfloat16), value...  13.5 us
    dot_general x8, matrix products, absorb(): jnp.einsum('rnkgd,rpkd->rnkgp', query_grid, key_block, preferred_element_...  11.7 us
    dot_general x1, matrix products, per_device(): jnp.dot(attended, lax.all_gather(out_weight, 'dp', axis=1, tiled=True), p...  8.12 us
    reduce_sum x8, other arithmetic, absorb(): new_sum = old_sum * rescale + jnp.sum(block_weights, axis=-1)  5.06 us
  transfers between devices with their start and end apart: 2, of which 2 were waited for; matrix products, arithmetic and copies ran while one was open for 15% of the time, Pallas kernels for 0%

commit v1 on v0

--- a/solution.py
+++ b/solution.py
@@ -124,7 +124,9 @@
     attended = attended.reshape(request_count * node_count, kv_local * group_size * HD)
     partial_sum = jnp.dot(
         attended,
-        lax.all_gather(out_weight, "dp", axis=1, tiled=True),
+        jnp.concatenate(
+            lax.all_to_all(jnp.stack([out_weight] * lax.axis_size("dp")), "dp", 0, 0), axis=1
+        ),
         preferred_element_type=jnp.float32,
     )
     own_share = summed_on_arrival(partial_sum.astype(jnp.bfloat16), "mp", 1)

time: 247 us -> 507 us (2.05)
  waiting for transfers between devices: 145 us -> 376 us
  blocking collectives: 34.5 us -> 55.8 us
  between operations: 14.3 us -> 0.9 us
  starting transfers between devices: 4.42 us -> 16.3 us
  local copies, waits for them, and re-layouts: 5.06 us -> 11.4 us
    all_to_all x0 -> x1, waiting for transfers between devices: none -> 349 us  [per_device(): lax.all_to_all(jnp.stack([out_weight] * lax.axis_size('dp')), 'dp', 0, 0)]
    all_gather x1 -> x0, waiting for transfers between devices: 117 us -> none  [per_device(): lax.all_gather(out_weight, 'dp', axis=1, tiled=True)]
    all_to_all x1, blocking collectives: 34.5 us -> 55.8 us  [sent_to_all(): lax.all_to_all(jnp.broadcast_to(value[None], (size, *value.shape)), axis,...]
    all_to_all x0 -> x1, starting transfers between devices: none -> 11.9 us  [per_device(): lax.all_to_all(jnp.stack([out_weight] * lax.axis_size('dp')), 'dp', 0, 0)]
    another operation x1 -> x2, local copies, waits for them, and re-layouts: 0.2 us -> 6.18 us  [the longest x1 5.99 us: per_device(): jnp.stack([out_weight] * lax.axis_size('dp'))]
  transfers between devices with their start and end apart: 2 -> 2, of which waited for: 2 -> 2; matrix products, arithmetic and copies ran while one was open for 15% -> 7% of each run, Pallas kernels for 0% -> 0%
where the time goes in v1:
time: 507 us; the launch traced here: 506 us
  waiting for transfers between devices  376 us (74%)
  blocking collectives  55.8 us (11%)
  matrix products  38.4 us (8%)
  starting transfers between devices  16.3 us (3%)
  local copies, waits for them, and re-layouts  11.4 us (2%)
  other arithmetic  6.76 us (1%)
    all_to_all x1, waiting for transfers between devices, per_device(): lax.all_to_all(jnp.stack([out_weight] * lax.axis_size('dp')), 'dp', 0, 0)  349 us
    all_to_all x1, blocking collectives, sent_to_all(): lax.all_to_all(jnp.broadcast_to(value[None], (size, *value.shape)), axis,...  55.8 us
    all_to_all x1, waiting for transfers between devices, summed_on_arrival(): lax.all_to_all(blocks, axis, split_axis=0, concat_axis=0, tiled=True)  26.9 us
    dot_general x8, matrix products, absorb(): jnp.einsum('rnkgp,rpkd->rnkgd', block_weights.astype(jnp.bfloat16), value...  13.5 us
    all_to_all x1, starting transfers between devices, per_device(): lax.all_to_all(jnp.stack([out_weight] * lax.axis_size('dp')), 'dp', 0, 0)  11.9 us
    dot_general x8, matrix products, absorb(): jnp.einsum('rnkgd,rpkd->rnkgp', query_grid, key_block, preferred_element_...  11.7 us
    dot_general x1, matrix products, per_device(): jnp.dot(attended, jnp.concatenate(lax.all_to_all(jnp.stack([out_weight] *...  11.4 us
  transfers between devices with their start and end apart: 2, of which 2 were waited for; matrix products, arithmetic and copies ran while one was open for 7% of the time, Pallas kernels for 0%

profile of v1, /device:TPU:8, one launch (start us, length us, event | category | flops | bytes accessed | tf_op | source)
XLA Modules:
  0.0 505.9 jit_solution(15325253362405561197)
XLA Ops:
  1.9 6.0 %stack.2 = bf16[32,1024,256]{1,2,0:T(8,128)(2,1)} broadcast(bf16[1024,256]{0,1:T(8,128)(2,1)S(1)} %copy.29), dimensions={1,2} | broadcast | bytes 17301504 | tf_op jit(solution)/shard_map/stack | solution.py:128
  7.9 11.9 %all-to-all-start = ((bf16[32,1024,256]{1,2,0:T(8,128)(2,1)}), bf16[32,1024,256]{1,2,0:T(8,128)(2,1)}, u32[]{:S(2)}, u32[]{:S(2)}) async-start(bf16[32,1024,256]{1,2,0:T(8,128)(2,1)} %stack.2), calls=%async_computation | async-start | bytes 33554432 | tf_op jit(solution)/shard_map/all_to_all | solution.py:128
  22.4 31.5 %while.17 = (s32[]{:T(128)}, f32[2,64,1,8]{1,3,0,2:T(8,128)S(1)}, f32[2,64,1,8]{1,3,0,2:T(8,128)S(1)}, f32[2,64,1,8,128]{4,1,3,0,2:T(8,128)S(1)}, s32[2]{0:T(128...) while((s32[]{:T(128)}, f32[2,64,1,8]{1,3,0,2:T(8,128)S(1)}, ...), condition=%wide.region_5.6_spmd, body=%wide.region_2.5_spmd.sunk | while | flops 274469376 | bytes 8200383 | solution.py:122
  24.7 1.7 fusion.60
  26.5 1.5 bitcast_reduce_fusion.2
  28.6 1.7 fusion.60
  30.4 1.5 bitcast_reduce_fusion.2
  32.5 1.7 fusion.60
  34.3 1.5 bitcast_reduce_fusion.2
  36.5 1.7 fusion.60
  38.3 1.5 bitcast_reduce_fusion.2
  40.4 1.7 fusion.60
  42.2 1.5 bitcast_reduce_fusion.2
  44.4 1.7 fusion.60
  46.2 1.5 bitcast_reduce_fusion.2
  48.3 1.7 fusion.60
  50.1 1.5 bitcast_reduce_fusion.2
  52.2 1.7 fusion.60
  54.3 348.9 %all-to-all-done = bf16[32,1024,256]{1,2,0:T(8,128)(2,1)} async-done(((bf16[32,1024,256]{1,2,0:T(8,128)(2,1)}), bf16[32,1024,256]{1,2,0:T(8,128)(2,1)}, u32[]{:S(2)}, u32[]{:S(2)}) %all-to-all-start) | async-done | bytes 16777248 | tf_op jit(solution)/shard_map/all_to_all | solution.py:128
  403.3 11.4 %convolution_convert_fusion = bf16[128,8192]{1,0:T(8,128)(2,1)S(1)} fusion(bf16[1024,8192]{0,1:T(8,128)(2,1)} %bitcast.34, bf16[16,8,8,128]{3,2,1,0:T(8,128)(2,1)S(1)} %bitcast.166), kind=kOutput, calls=%fused_computation.30 | convolution fusion | flops 2148532224 | bytes 19136512 | tf_op jit(solution)/shard_map/dot_general | solution.py:125
  414.7 1.6 copy.48
  416.3 4.4 all-to-all-start.1
  421.0 26.9 %all-to-all-done.1 = bf16[8,128,1024]{2,1,0:T(8,128)(2,1)S(1)} async-done(((bf16[8,128,1024]{2,1,0:T(8,128)(2,1)}), bf16[8,128,1024]{2,1,0:T(8,128)(2,1)S(1)}, u32[]{:S(2)}, u32[]{:S(2)}) %all-to-all-start.1) | async-done | bytes 2097184 | tf_op jit(solution)/shard_map/all_to_all | solution.py:20
  449.1 55.8 %all_to_all.15 = bf16[32,16,1024]{2,1,0:T(8,128)(2,1)S(1)} all-to-all(bf16[32,16,1024]{2,1,0:T(8,128)(2,1)S(1)} %broadcast_in_dim.78), channel_id=1, replica_groups=mesh['dp'=32,'mp'=8] {'dp'}, dimensions={0} | all-to-all | bytes 2097152 | tf_op jit(solution)/shard_map/all_to_all | solution.py:26
  (96 shorter events, 13.9 us)
Async XLA Ops:
  0.6 21.4 %copy-start = (bf16[128,128]{1,0:T(8,128)(2,1)S(1)}, bf16[128,128]{1,0:T(8,128)(2,1)}, u32[]{:S(2)}) copy-start(bf16[128,128]{1,0:T(8,128)(2,1)} %param.14) | copy-start | bytes 98308
  7.9 11.9 %copy-start.2 = (bf16[128,1024]{1,0:T(8,128)(2,1)S(1)}, bf16[128,1024]{1,0:T(8,128)(2,1)}, u32[]{:S(2)}) copy-start(bf16[128,1024]{1,0:T(8,128)(2,1)} %param.12) | copy-start | bytes 786436
  7.9 12.0 %copy-start.6 = (s32[2,64]{1,0:T(2,128)S(1)}, s32[2,64]{1,0:T(2,128)}, u32[]{:S(2)}) copy-start(s32[2,64]{1,0:T(2,128)} %param.18) | copy-start | bytes 1540
  7.9 13.4 %copy-start.4 = (bf16[128,128]{1,0:T(8,128)(2,1)S(1)}, bf16[128,128]{1,0:T(8,128)(2,1)}, u32[]{:S(2)}) copy-start(bf16[128,128]{1,0:T(8,128)(2,1)} %param.13) | copy-start | bytes 98308
  7.9 395.4 %all-to-all-start = ((bf16[32,1024,256]{1,2,0:T(8,128)(2,1)}), bf16[32,1024,256]{1,2,0:T(8,128)(2,1)}, u32[]{:S(2)}, u32[]{:S(2)}) async-start(bf16[32,1024,256]{1,2,0:T(8,128)(2,1)} %stack.2), calls=%async_computation | async-start | bytes 33554432 | tf_op jit(solution)/shard_map/all_to_all | solution.py:128
  21.3 1.1 copy-start.5
  416.3 4.4 copy-start.7
  416.3 31.6 %all-to-all-start.1 = ((bf16[8,128,1024]{2,1,0:T(8,128)(2,1)}), bf16[8,128,1024]{2,1,0:T(8,128)(2,1)S(1)}, u32[]{:S(2)}, u32[]{:S(2)}) async-start(bf16[8,128,1024]{2,1,0:T(8,128)(2,1)} %bitcast.159), calls=%async_computation.1 | async-start | bytes 4194304 | tf_op jit(solution)/shard_map/all_to_all | solution.py:20
  420.7 27.5 %copy-start.3 = (bf16[128,1024]{1,0:T(8,128)(2,1)S(1)}, bf16[128,1024]{1,0:T(8,128)(2,1)}, u32[]{:S(2)}) copy-start(bf16[128,1024]{1,0:T(8,128)(2,1)} %param.20) | copy-start | bytes 786436
  448.3 57.6 %copy-start.1 = (bf16[128,1024]{1,0:T(8,128)(2,1)}, bf16[128,1024]{1,0:T(8,128)(2,1)S(1)}, u32[]{:S(2)}) copy-start(bf16[128,1024]{1,0:T(8,128)(2,1)S(1)} %add_convert_fusion) | copy-start | bytes 786436
